TPU v7x, 32 devices: a whole 2x2x4 slice. The times are simulated.
32 devices in a mesh: gx: 4 (over y, x), gy: 4 (over z), gz: 2 (over core).
Axes of the slice: x: 2, y: 2, z: 4, core: 2. Of those that a mesh axis runs over, the one named last changes fastest.
Arguments:
- element_load: float32 [36, 36, 18, 128], P('gx', 'gy', 'gz'), may hold values from -90 to 90
- local_matrix: float32 [4, 4, 2, 729, 729], P('gx', 'gy', 'gz'), may hold values from -10 to 61, as said below
- dirichlet_inverse: float32 [4, 4, 2, 343, 343], P('gx', 'gy', 'gz'), as said below
- neumann_inverse: float32 [4, 4, 2, 729, 729], P('gx', 'gy', 'gz'), as said below
- coarse_basis: float32 [4, 4, 2, 20, 729], P('gx', 'gy', 'gz'), as said below
Outputs:
- solution: float32 [36, 36, 18, 128], P('gx', 'gy', 'gz')
- residual: float32 [36, 36, 18, 128], P('gx', 'gy', 'gz')
Inputs may be any that keep to these rules, and one draw needn't show every extreme that they name: `local_matrix`: block (a, b, c) is the symmetric positive definite stiffness matrix of subdomain (a, b, c) in the node order of the steps: cellwise conductivities on the couplings of neighbouring nodes plus a lumped reaction term. `dirichlet_inverse`: block (a, b, c) is the inverse, computed in float32, of local_matrix's block restricted to the inner nodes. `neumann_inverse`: block (a, b, c) is the node-by-node block of the inverse, computed in float32, of the saddle-point matrix [[A, Cm^T], [Cm, 0]], with A local_matrix's block and Cm the 20 x 729 primal constraints in the order of the coarse numbering: the value at each of the 8 corners, then the mean over the 7 inner nodes of each of the 12 edges. `coarse_basis`: block (a, b, c) is the constraint-by-node block of that same saddle-point inverse.
All inputs are finite; a program needn't handle non-finite values.
Results may differ from a plain program's by a relative error of at most 0.0014.
Values sent between devices are 32-bit elements; how exact they have to be, the bound alone decides.
No kernel may reach another device: no remote copies, remote signals or barrier semaphores. Data moves between devices by JAX's collectives and lax.ppermute only.
A program may use at most 128 MiB of HBM per device.

v0:
```python
import jax
import jax.numpy as jnp
from jax import lax
from jax.sharding import PartitionSpec as P

ITERS = 2


def with_halo(array, sides, width):
    for axis, dim in sides:
        size, length = (lax.axis_size(axis), array.shape[dim])
        up = [(i, (i + 1) % size) for i in range(size)]
        down = [(j, i) for i, j in up]
        last = lax.slice_in_dim(array, length - width, length, axis=dim)
        leading = lax.slice_in_dim(array, 0, width, axis=dim)
        before = lax.ppermute(last, axis, up)
        after = lax.ppermute(leading, axis, down)
        array = jnp.concatenate([before, array, after], axis=dim)
    return array


def matmul(left_side, right_side):
    return jnp.dot(
        left_side, right_side, precision=lax.Precision.HIGHEST, preferred_element_type=jnp.float32
    )


def coarse_ids(along_x, along_y, along_z, count_x, count_y, count_z):
    total = count_x * count_y * count_z

    def vertex(shift_x, shift_y, shift_z):
        return (
            (along_x + shift_x) % count_x * count_y + (along_y + shift_y) % count_y
        ) * count_z + (along_z + shift_z) % count_z

    listed = [vertex(sx, sy, sz) for sx in (0, 1) for sy in (0, 1) for sz in (0, 1)]
    listed += [total + vertex(0, sy, sz) for sy in (0, 1) for sz in (0, 1)]
    listed += [2 * total + vertex(sx, 0, sz) for sx in (0, 1) for sz in (0, 1)]
    listed += [3 * total + vertex(sx, sy, 0) for sx in (0, 1) for sy in (0, 1)]
    return jnp.stack(listed, axis=-1)


def node_weights(node_side):
    places = jnp.arange(node_side, dtype=jnp.int32)
    on_rim = ((places == 0) | (places == node_side - 1)).astype(jnp.int32)
    rims = on_rim[:, None, None] + on_rim[None, :, None] + on_rim[None, None, :]
    copies = (
        (1.0 + on_rim[:, None, None].astype(jnp.float32))
        * (1.0 + on_rim[None, :, None].astype(jnp.float32))
        * (1.0 + on_rim[None, None, :].astype(jnp.float32))
    )
    share = (1.0 / copies)[..., None]
    border = jnp.where(rims[..., None] > 0, share, jnp.zeros_like(share))
    return (share, border)


def fold_rim(padded, axis_dim):
    length = padded.shape[axis_dim]
    inside = lax.slice_in_dim(padded, 1, length - 1, axis=axis_dim)
    lowest = lax.slice_in_dim(padded, 0, 1, axis=axis_dim)
    highest = lax.slice_in_dim(padded, length - 1, length, axis=axis_dim)
    middle_shape = list(lowest.shape)
    middle_shape[axis_dim] = length - 4
    addend = jnp.concatenate(
        [lowest, jnp.zeros(middle_shape, padded.dtype), highest], axis=axis_dim
    )
    return inside + addend


def local(element_load, local_matrix, dirichlet_inverse, neumann_inverse, coarse_basis):
    highest_prec = lax.Precision.HIGHEST
    node_side = element_load.shape[0]
    rhs_count = element_load.shape[3]
    node_count = node_side**3
    inner_side = node_side - 2
    inner_count = inner_side**3
    primal = coarse_basis.shape[3]
    stiffness = local_matrix.reshape(node_count, node_count)
    interior_inverse = dirichlet_inverse.reshape(inner_count, inner_count)
    neumann = neumann_inverse.reshape(node_count, node_count)
    basis = coarse_basis.reshape(primal, node_count)
    stiff_cols = stiffness.reshape(node_count, node_side, node_side, node_side)[
        :, 1:-1, 1:-1, 1:-1
    ].reshape(node_count, inner_count)
    stiff_rows = stiffness.reshape(node_side, node_side, node_side, node_count)[
        1:-1, 1:-1, 1:-1
    ].reshape(inner_count, node_count)
    share, border = node_weights(node_side)
    count_x = lax.axis_size("gx")
    count_y = lax.axis_size("gy")
    count_z = lax.axis_size("gz")
    coarse_count = 4 * count_x * count_y * count_z
    own_ids = coarse_ids(
        lax.axis_index("gx"), lax.axis_index("gy"), lax.axis_index("gz"), count_x, count_y, count_z
    )
    columns = jnp.arange(coarse_count, dtype=jnp.int32)
    own_indicator = (own_ids[:, None] == columns[None, :]).astype(jnp.float32)
    coarse_local = matmul(basis, matmul(stiffness, basis.T))

    def piece_indicator(count_rows):
        linear = jnp.arange(count_rows, dtype=jnp.int32)
        piece_ids = coarse_ids(
            linear // (count_y * count_z),
            linear // count_z % count_y,
            linear % count_z,
            count_x,
            count_y,
            count_z,
        )
        return (piece_ids[:, :, None] == columns[None, None, :]).astype(jnp.float32)

    received = lax.all_gather(coarse_local[None], ("gx", "gy", "gz"), axis=0, tiled=True)
    indicator = piece_indicator(received.shape[0])
    partial_rows = jnp.einsum("zpm,zpq->zmq", indicator, received, precision=highest_prec)
    coarse_matrix = jnp.einsum("zmq,zqn->mn", partial_rows, indicator, precision=highest_prec)
    factor = jnp.linalg.cholesky(coarse_matrix)

    def coarse_rhs(primal_load):
        received = lax.all_gather(primal_load[None], ("gx", "gy", "gz"), axis=0, tiled=True)
        indicator = piece_indicator(received.shape[0])
        return jnp.einsum("zpm,zpk->mk", indicator, received, precision=highest_prec)

    def assemble(field):
        padded = with_halo(field, (("gx", 0),), 1)
        field = fold_rim(padded, 0)
        padded = with_halo(field, (("gy", 1),), 1)
        field = fold_rim(padded, 1)
        padded = with_halo(field, (("gz", 2),), 1)
        result_field = fold_rim(padded, 2)
        return result_field

    cube_shape = (node_side, node_side, node_side, rhs_count)

    def precondition(current):
        inner_part = current[1:-1, 1:-1, 1:-1].reshape(inner_count, rhs_count)
        start = matmul(interior_inverse, inner_part)
        spill = matmul(stiff_cols, start).reshape(cube_shape)
        first_residual = current - assemble(spill)
        weighted = (border * first_residual).reshape(node_count, rhs_count)
        local_part = matmul(neumann, weighted)
        primal_load = matmul(basis, weighted)
        coarse_values = jax.scipy.linalg.cho_solve((factor, True), coarse_rhs(primal_load))
        primal_values = matmul(own_indicator, coarse_values)
        combined = local_part + matmul(basis.T, primal_values)
        surface = assemble(border * combined.reshape(cube_shape))
        inner_new = start - matmul(
            interior_inverse, matmul(stiff_rows, surface.reshape(node_count, rhs_count))
        )
        padded_inner = jnp.pad(
            inner_new.reshape(inner_side, inner_side, inner_side, rhs_count),
            ((1, 1), (1, 1), (1, 1), (0, 0)),
        )
        return surface + padded_inner

    right_side = assemble(element_load)
    solution = jnp.zeros(cube_shape, jnp.float32)
    residual = right_side

    def precond_dot(left_field, right_field):
        return lax.psum(
            jnp.sum(left_field * right_field * share, axis=(0, 1, 2)), ("gx", "gy", "gz")
        )

    precond_now = precondition(residual)
    direction = precond_now
    energy = precond_dot(residual, precond_now)
    for iteration in range(ITERS):
        mapped = assemble(
            matmul(stiffness, direction.reshape(node_count, rhs_count)).reshape(cube_shape)
        )
        step_size = energy / lax.psum(
            jnp.sum(direction * mapped * share, axis=(0, 1, 2)), ("gx", "gy", "gz")
        )
        solution = solution + step_size * direction
        residual = residual - step_size * mapped
        if iteration + 1 < ITERS:
            precond_now = precondition(residual)
            energy_next = precond_dot(residual, precond_now)
            direction = precond_now + energy_next / energy * direction
            energy = energy_next
    return (solution, residual)


def solution(mesh):
    in_specs = (
        P("gx", "gy", "gz", None),
        P("gx", "gy", "gz", None, None),
        P("gx", "gy", "gz", None, None),
        P("gx", "gy", "gz", None, None),
        P("gx", "gy", "gz", None, None),
    )
    out_specs = (P("gx", "gy", "gz", None), P("gx", "gy", "gz", None))
    return jax.shard_map(local, mesh=mesh, in_specs=in_specs, out_specs=out_specs, check_vma=False)
```

profile of v0, /device:TPU:10, one launch (start us, length us, event | category | flops | bytes accessed | tf_op | source)
XLA Modules:
  0.0 518.0 jit_solution(8985004358485511838)
XLA Ops:
  4.9 3.7 fusion.4
  8.9 34.8 %all-gather.3 = f32[32,20,20]{2,1,0:T(8,128)S(1)} all-gather(f32[1,20,20]{2,1,0:T(8,128)S(1)} %copy.11), channel_id=2, replica_groups=mesh['gx'=4,'gy'=4,'gz'=2] {'gx','gy','gz'}, dimensions={0}, use_global_device_ids=true | all-gather | bytes 52800 | tf_op jit(solution)/shard_map/all_gather | solution.py:112
  46.4 3.1 collective-permute-start.3
  51.9 5.0 collective-permute-done.2
  58.9 5.0 copy.10
  63.9 3.7 reshape_reshape.6
  72.7 13.2 %cholesky.18 = f32[128,128]{1,0:T(8,128)} custom-call(f32[128,128]{1,0:T(8,128)} %fusion.80), custom_call_target="Cholesky" | custom-call | tf_op jit(solution)/shard_map/jit(cholesky)/cholesky | solution.py:116
  91.1 3.3 convolution_bitcast_fusion.1
  97.2 4.0 collective-permute-start.7
  119.0 11.3 %custom-call.9 = f32[1,128,128]{1,2,0:T(8,128)} custom-call(f32[1,128,128]{2,1,0:T(8,128)} %fusion.71), custom_call_target="InvertDiagBlocksLowerTriangular" | custom-call | tf_op jit(solution)/shard_map/jit(_cho_solve)/triangular_solve | solution.py:142
  136.7 3.7 fusion.8
  140.4 36.0 %all-gather.4 = f32[32,20,128]{2,1,0:T(8,128)S(1)} all-gather(f32[1,20,128]{2,1,0:T(8,128)S(1)} %convolution_bitcast_fusion.7), channel_id=3, replica_groups=mesh['gx'=4,'gy'=4,'gz'=2] {'gx','gy','gz'}, dimensions={0}, use_global_device_ids=true | all-gather | bytes 337920 | tf_op jit(solution)/shard_map/all_gather | solution.py:119
  182.5 4.5 collective-permute-start.13
  203.2 7.4 %reduce.6 = f32[729,729]{1,0:T(8,128)} reduce(f32[1,1,1,729,729]{4,2,3,1,0:T(1,128)S(1)} %copy-done, f32[]{:T(128)} %constant.929), dimensions={0,1,2}, to_apply=%param.8.reduce_sub_computation | reduce | bytes 4251532 | tf_op args[1]
  210.6 3.7 reshape_reshape.7
  254.8 3.0 collective-permute-done.21
  263.9 41.8 %all-reduce.2 = (f32[128]{0:T(128)}, f32[128]{0:T(128)}) all-reduce(f32[128]{0:T(128)} %get-tuple-element.4, f32[128]{0:T(128)} %get-tuple-element.3), channel_id=1, replica_groups=mesh['gx'=4,'gy'=4,'gz'=2] {'gx','gy','gz'}, use_global_device_ids=true, to_apply=%region_3.5 | all-reduce | flops 256 | bytes 2048 | tf_op jit(solution)/shard_map/psum | solution.py:160
  309.7 3.4 convolution_bitcast_fusion
  332.1 3.6 fusion.6
  336.1 37.3 %all-gather.5 = f32[32,20,128]{2,1,0:T(8,128)S(1)} all-gather(f32[1,20,128]{2,1,0:T(8,128)S(1)} %convolution_bitcast_fusion.6), channel_id=4, replica_groups=mesh['gx'=4,'gy'=4,'gz'=2] {'gx','gy','gz'}, dimensions={0}, use_global_device_ids=true | all-gather | bytes 337920 | tf_op jit(solution)/shard_map/all_gather | solution.py:119
  377.5 6.4 %collective-permute-start.31 = (f32[1,9,9,128]{3,2,1,0:T(8,128)S(1)}, f32[1,9,9,128]{3,2,1,0:T(8,128)S(1)}, u32[]{:S(2)}, u32[]{:S(2)}) collective-permute-start(f32[1,9,9,128]{3,2,1,0:T(8,128)S(1)} %get-tuple-element.16), channel_id=1, source_target_pairs={{8,0},{16,8},{24,16},{0,24},{9,1},{17,9},{25,17},{1,25},{10,2},{18... | collective-permute-start | bytes 124424 | tf_op jit(solution)/shard_map/ppermute | solution.py:17
  410.6 42.3 %psum.30 = f32[128]{0:T(128)S(1)} all-reduce(f32[128]{0:T(128)S(1)} %multiply_reduce_fusion.1), channel_id=1, replica_groups=mesh['gx'=4,'gy'=4,'gz'=2] {'gx','gy','gz'}, use_global_device_ids=true, to_apply=%region_7.9 | all-reduce | flops 128 | bytes 1024 | tf_op jit(solution)/shard_map/psum | solution.py:160
  460.6 2.9 collective-permute-start.36
  473.2 43.2 %psum.31 = f32[128]{0:T(128)S(1)} all-reduce(f32[128]{0:T(128)S(1)} %multiply_reduce_fusion), channel_id=1, replica_groups=mesh['gx'=4,'gy'=4,'gz'=2] {'gx','gy','gz'}, use_global_device_ids=true, to_apply=%region_9.11 | all-reduce | flops 128 | bytes 1024 | tf_op jit(solution)/shard_map/psum | solution.py:171
  (317 shorter events, 189.9 us)
Async XLA Ops:
  1.6 44.6 %collective-permute-start.1 = (f32[1,9,9,128]{3,2,1,0:T(8,128)S(1)}, f32[1,9,9,128]{3,2,1,0:T(8,128)S(1)}, u32[]{:S(2)}, u32[]{:S(2)}) collective-permute-start(f32[1,9,9,128]{3,2,1,0:T(8,128)S(1)} %get-tuple-element.40), channel_id=1, source_target_pairs={{8,0},{16,8},{24,16},{0,24},{9,1},{17,9},{25,17},{1,25},{10,2},{18... | collective-permute-start | bytes 124424 | tf_op jit(solution)/shard_map/ppermute | solution.py:17
  2.2 44.1 %collective-permute-start = (f32[1,9,9,128]{3,2,1,0:T(8,128)S(1)}, f32[1,9,9,128]{3,2,1,0:T(8,128)S(1)}, u32[]{:S(2)}, u32[]{:S(2)}) collective-permute-start(f32[1,9,9,128]{3,2,1,0:T(8,128)S(1)} %get-tuple-element.39), channel_id=1, source_target_pairs={{0,8},{8,16},{16,24},{24,0},{1,9},{9,17},{17,25},{25,1},{2,10},{10... | collective-permute-start | bytes 124424 | tf_op jit(solution)/shard_map/ppermute | solution.py:16
  46.4 5.5 %collective-permute-start.3 = (f32[9,1,9,128]{3,2,1,0:T(8,128)S(1)}, f32[9,1,9,128]{3,2,1,0:T(8,128)S(1)}, u32[]{:S(2)}, u32[]{:S(2)}) collective-permute-start(f32[9,1,9,128]{3,2,1,0:T(8,128)S(1)} %get-tuple-element.38), channel_id=1, source_target_pairs={{2,0},{4,2},{6,4},{0,6},{3,1},{5,3},{7,5},{1,7},{10,8},{12,10},{14... | collective-permute-start | bytes 124424 | tf_op jit(solution)/shard_map/ppermute | solution.py:17
  49.5 7.3 %collective-permute-start.2 = (f32[9,1,9,128]{3,2,1,0:T(8,128)S(1)}, f32[9,1,9,128]{3,2,1,0:T(8,128)S(1)}, u32[]{:S(2)}, u32[]{:S(2)}) collective-permute-start(f32[9,1,9,128]{3,2,1,0:T(8,128)S(1)} %get-tuple-element.37), channel_id=1, source_target_pairs={{0,2},{2,4},{4,6},{6,0},{1,3},{3,5},{5,7},{7,1},{8,10},{10,12},{12... | collective-permute-start | bytes 124424 | tf_op jit(solution)/shard_map/ppermute | solution.py:16
  57.7 28.2 %collective-permute-start.5 = (f32[9,9,1,128]{3,2,1,0:T(1,128)}, f32[9,9,1,128]{3,2,1,0:T(1,128)S(1)}, u32[]{:S(2)}, u32[]{:S(2)}) collective-permute-start(f32[9,9,1,128]{3,2,1,0:T(1,128)} %get-tuple-element.36), channel_id=1, source_target_pairs={{1,0},{0,1},{3,2},{2,3},{5,4},{4,5},{7,6},{6,7},{9,8},{8,9},{11,10... | collective-permute-start | bytes 124424 | tf_op jit(solution)/shard_map/ppermute | solution.py:17
  57.7 28.2 %collective-permute-start.4 = (f32[9,9,1,128]{3,2,1,0:T(1,128)}, f32[9,9,1,128]{3,2,1,0:T(1,128)}, u32[]{:S(2)}, u32[]{:S(2)}) collective-permute-start(f32[9,9,1,128]{3,2,1,0:T(1,128)} %get-tuple-element.35), channel_id=1, source_target_pairs={{0,1},{1,0},{2,3},{3,2},{4,5},{5,4},{6,7},{7,6},{8,9},{9,8},{10,11... | collective-permute-start | bytes 124424 | tf_op jit(solution)/shard_map/ppermute | solution.py:16
  97.2 8.7 %collective-permute-start.7 = (f32[1,9,9,128]{3,2,1,0:T(8,128)}, f32[1,9,9,128]{3,2,1,0:T(8,128)}, u32[]{:S(2)}, u32[]{:S(2)}) collective-permute-start(f32[1,9,9,128]{3,2,1,0:T(8,128)} %slice.187), channel_id=1, source_target_pairs={{8,0},{16,8},{24,16},{0,24},{9,1},{17,9},{25,17},{1,25},{10,2},{18... | collective-permute-start | bytes 124424 | tf_op jit(solution)/shard_map/ppermute | solution.py:17
  102.7 4.7 collective-permute-start.6
  108.6 5.1 collective-permute-start.9
  117.2 13.7 %collective-permute-start.11 = (f32[9,9,1,128]{3,2,1,0:T(1,128)}, f32[9,9,1,128]{3,2,1,0:T(1,128)}, u32[]{:S(2)}, u32[]{:S(2)}) collective-permute-start(f32[9,9,1,128]{3,2,1,0:T(1,128)} %get-tuple-element.32), channel_id=1, source_target_pairs={{1,0},{0,1},{3,2},{2,3},{5,4},{4,5},{7,6},{6,7},{9,8},{8,9},{11,10... | collective-permute-start | bytes 124424 | tf_op jit(solution)/shard_map/ppermute | solution.py:17
  117.2 13.7 %collective-permute-start.10 = (f32[9,9,1,128]{3,2,1,0:T(1,128)}, f32[9,9,1,128]{3,2,1,0:T(1,128)}, u32[]{:S(2)}, u32[]{:S(2)}) collective-permute-start(f32[9,9,1,128]{3,2,1,0:T(1,128)} %get-tuple-element.31), channel_id=1, source_target_pairs={{0,1},{1,0},{2,3},{3,2},{4,5},{5,4},{6,7},{7,6},{8,9},{9,8},{10,11... | collective-permute-start | bytes 124424 | tf_op jit(solution)/shard_map/ppermute | solution.py:16
  182.5 7.6 %collective-permute-start.13 = (f32[1,9,9,128]{3,2,1,0:T(8,128)S(1)}, f32[1,9,9,128]{3,2,1,0:T(8,128)S(1)}, u32[]{:S(2)}, u32[]{:S(2)}) collective-permute-start(f32[1,9,9,128]{3,2,1,0:T(8,128)S(1)} %get-tuple-element.30), channel_id=1, source_target_pairs={{8,0},{16,8},{24,16},{0,24},{9,1},{17,9},{25,17},{1,25},{10,2},{18... | collective-permute-start | bytes 124424 | tf_op jit(solution)/shard_map/ppermute | solution.py:17
  202.0 21.0 %collective-permute-start.17 = (f32[9,9,1,128]{3,2,1,0:T(1,128)}, f32[9,9,1,128]{3,2,1,0:T(1,128)}, u32[]{:S(2)}, u32[]{:S(2)}) collective-permute-start(f32[9,9,1,128]{3,2,1,0:T(1,128)} %get-tuple-element.26), channel_id=1, source_target_pairs={{1,0},{0,1},{3,2},{2,3},{5,4},{4,5},{7,6},{6,7},{9,8},{8,9},{11,10... | collective-permute-start | bytes 124424 | tf_op jit(solution)/shard_map/ppermute | solution.py:17
  202.0 21.0 %collective-permute-start.16 = (f32[9,9,1,128]{3,2,1,0:T(1,128)}, f32[9,9,1,128]{3,2,1,0:T(1,128)}, u32[]{:S(2)}, u32[]{:S(2)}) collective-permute-start(f32[9,9,1,128]{3,2,1,0:T(1,128)} %get-tuple-element.25), channel_id=1, source_target_pairs={{0,1},{1,0},{2,3},{3,2},{4,5},{5,4},{6,7},{7,6},{8,9},{9,8},{10,11... | collective-permute-start | bytes 124424 | tf_op jit(solution)/shard_map/ppermute | solution.py:16
  242.3 6.6 %collective-permute-start.19 = (f32[1,9,9,128]{3,2,1,0:T(8,128)}, f32[1,9,9,128]{3,2,1,0:T(8,128)}, u32[]{:S(2)}, u32[]{:S(2)}) collective-permute-start(f32[1,9,9,128]{3,2,1,0:T(8,128)} %slice.202), channel_id=1, source_target_pairs={{8,0},{16,8},{24,16},{0,24},{9,1},{17,9},{25,17},{1,25},{10,2},{18... | collective-permute-start | bytes 124424 | tf_op jit(solution)/shard_map/ppermute | solution.py:17
  246.4 5.1 collective-permute-start.18
  252.7 5.1 collective-permute-start.21
  313.8 5.6 %collective-permute-start.25 = (f32[1,9,9,128]{3,2,1,0:T(8,128)}, f32[1,9,9,128]{3,2,1,0:T(8,128)}, u32[]{:S(2)}, u32[]{:S(2)}) collective-permute-start(f32[1,9,9,128]{3,2,1,0:T(8,128)} %slice.211), channel_id=1, source_target_pairs={{8,0},{16,8},{24,16},{0,24},{9,1},{17,9},{25,17},{1,25},{10,2},{18... | collective-permute-start | bytes 124424 | tf_op jit(solution)/shard_map/ppermute | solution.py:17
  314.5 5.5 %collective-permute-start.24 = (f32[1,9,9,128]{3,2,1,0:T(8,128)}, f32[1,9,9,128]{3,2,1,0:T(8,128)}, u32[]{:S(2)}, u32[]{:S(2)}) collective-permute-start(f32[1,9,9,128]{3,2,1,0:T(8,128)} %slice.209), channel_id=1, source_target_pairs={{0,8},{8,16},{16,24},{24,0},{1,9},{9,17},{17,25},{25,1},{2,10},{10... | collective-permute-start | bytes 124424 | tf_op jit(solution)/shard_map/ppermute | solution.py:16
  377.5 9.2 %collective-permute-start.31 = (f32[1,9,9,128]{3,2,1,0:T(8,128)S(1)}, f32[1,9,9,128]{3,2,1,0:T(8,128)S(1)}, u32[]{:S(2)}, u32[]{:S(2)}) collective-permute-start(f32[1,9,9,128]{3,2,1,0:T(8,128)S(1)} %get-tuple-element.16), channel_id=1, source_target_pairs={{8,0},{16,8},{24,16},{0,24},{9,1},{17,9},{25,17},{1,25},{10,2},{18... | collective-permute-start | bytes 124424 | tf_op jit(solution)/shard_map/ppermute | solution.py:17
  389.8 5.1 collective-permute-start.32
  460.5 5.3 %collective-permute-start.37 = (f32[1,9,9,128]{3,2,1,0:T(8,128)S(1)}, f32[1,9,9,128]{3,2,1,0:T(8,128)S(1)}, u32[]{:S(2)}, u32[]{:S(2)}) collective-permute-start(f32[1,9,9,128]{3,2,1,0:T(8,128)S(1)} %slice.225), channel_id=1, source_target_pairs={{8,0},{16,8},{24,16},{0,24},{9,1},{17,9},{25,17},{1,25},{10,2},{18... | collective-permute-start | bytes 124424 | tf_op jit(solution)/shard_map/ppermute | solution.py:17
  460.6 5.3 %collective-permute-start.36 = (f32[1,9,9,128]{3,2,1,0:T(8,128)S(1)}, f32[1,9,9,128]{3,2,1,0:T(8,128)S(1)}, u32[]{:S(2)}, u32[]{:S(2)}) collective-permute-start(f32[1,9,9,128]{3,2,1,0:T(8,128)S(1)} %slice.223), channel_id=1, source_target_pairs={{0,8},{8,16},{16,24},{24,0},{1,9},{9,17},{17,25},{25,1},{2,10},{10... | collective-permute-start | bytes 124424 | tf_op jit(solution)/shard_map/ppermute | solution.py:16
  466.2 5.0 collective-permute-start.38
  (70 other events, 876.4 us)
where the time goes:
time: 524 us; the launch traced here: 518 us
  blocking collectives  235 us (45%)
  other arithmetic  73.6 us (14%)
  local copies, waits for them, and re-layouts  71.8 us (14%)
  starting transfers between devices  47.7 us (9%)
  waiting for transfers between devices  45 us (9%)
  matrix products  42.8 us (8%)
    psum x2, blocking collectives, precond_dot(): lax.psum(jnp.sum(left_field * right_field * share, axis=(0, 1, 2)), ('gx'...  84.1 us
    all_gather x2, blocking collectives, coarse_rhs(): lax.all_gather(primal_load[None], ('gx', 'gy', 'gz'), axis=0, tiled=True)  73.3 us
    psum x1, blocking collectives, local(): lax.psum(jnp.sum(direction * mapped * share, axis=(0, 1, 2)), ('gx', 'gy'...  43.2 us
    dot_general x20, matrix products, matmul(): jnp.dot(left_side, right_side, precision=lax.Precision.HIGHEST, preferred...  39.7 us
    all_gather x1, blocking collectives, local(): lax.all_gather(coarse_local[None], ('gx', 'gy', 'gz'), axis=0, tiled=True)  34.8 us
    ppermute x21, starting transfers between devices, with_halo(): after = lax.ppermute(leading, axis, down)  27.8 us
    ppermute x21, waiting for transfers between devices, with_halo(): after = lax.ppermute(leading, axis, down)  25.5 us
    ppermute x21, starting transfers between devices, with_halo(): before = lax.ppermute(last, axis, up)  19.9 us
  transfers between devices with their start and end apart: 42, of which 30 were waited for; matrix products, arithmetic and copies ran while one was open for 16% of the time, Pallas kernels for 0%

commit v1 on v0

--- a/solution.py
+++ b/solution.py
@@ -4,6 +4,12 @@
 from jax.sharding import PartitionSpec as P
 
 ITERS = 2
+
+
+def summed_here(x, mesh_axis):
+    parts = lax.all_gather(x, mesh_axis, axis=0, tiled=False)
+    result = parts.sum(axis=0)
+    return result
 
 
 def with_halo(array, sides, width):
@@ -157,7 +163,7 @@
     residual = right_side
 
     def precond_dot(left_field, right_field):
-        return lax.psum(
+        return summed_here(
             jnp.sum(left_field * right_field * share, axis=(0, 1, 2)), ("gx", "gy", "gz")
         )
 

time: 524 us -> 561 us (1.071)
  blocking collectives: 235 us -> 266 us
    psum x2 -> x0, blocking collectives: 84.1 us -> none  [precond_dot(): lax.psum(jnp.sum(left_field * right_field * share, axis=(0, 1, 2)), ('gx'...]
    all_gather x0 -> x2, blocking collectives: none -> 72.1 us  [summed_here(): parts = lax.all_gather(x, mesh_axis, axis=0, tiled=False)]
    psum x1 -> x2, blocking collectives: 43.2 us -> 85.8 us  [local(): lax.psum(jnp.sum(direction * mapped * share, axis=(0, 1, 2)), ('gx', 'gy'...]
    ppermute x21, starting transfers between devices: 27.8 us -> 35 us  [with_halo(): after = lax.ppermute(leading, axis, down)]
  transfers between devices with their start and end apart: 42 -> 42, of which waited for: 30 -> 30; matrix products, arithmetic and copies ran while one was open for 16% -> 15% of each run, Pallas kernels for 0% -> 0%
where the time goes in v1:
time: 561 us; the launch traced here: 555 us
  blocking collectives  266 us (47%)
  other arithmetic  74.9 us (13%)
  local copies, waits for them, and re-layouts  71.8 us (13%)
  starting transfers between devices  50.9 us (9%)
  waiting for transfers between devices  47.1 us (8%)
  matrix products  42.8 us (8%)
    psum x2, blocking collectives, local(): lax.psum(jnp.sum(direction * mapped * share, axis=(0, 1, 2)), ('gx', 'gy'...  85.8 us
    all_gather x2, blocking collectives, coarse_rhs(): lax.all_gather(primal_load[None], ('gx', 'gy', 'gz'), axis=0, tiled=True)  73.4 us
    all_gather x2, blocking collectives, summed_here(): parts = lax.all_gather(x, mesh_axis, axis=0, tiled=False)  72.1 us
    dot_general x20, matrix products, matmul(): jnp.dot(left_side, right_side, precision=lax.Precision.HIGHEST, preferred...  39.7 us
    ppermute x21, starting transfers between devices, with_halo(): after = lax.ppermute(leading, axis, down)  35 us
    all_gather x1, blocking collectives, local(): lax.all_gather(coarse_local[None], ('gx', 'gy', 'gz'), axis=0, tiled=True)  34.8 us
    ppermute x21, waiting for transfers between devices, with_halo(): after = lax.ppermute(leading, axis, down)  26.7 us
    ppermute x21, waiting for transfers between devices, with_halo(): before = lax.ppermute(last, axis, up)  20.4 us
  transfers between devices with their start and end apart: 42, of which 30 were waited for; matrix products, arithmetic and copies ran while one was open for 15% of the time, Pallas kernels for 0%

profile of v1, /device:TPU:10, one launch (start us, length us, event | category | flops | bytes accessed | tf_op | source)
XLA Modules:
  0.0 555.2 jit_solution(17163727876763686867)
XLA Ops:
  4.9 3.7 fusion.4
  8.9 34.8 %all-gather.5 = f32[32,20,20]{2,1,0:T(8,128)S(1)} all-gather(f32[1,20,20]{2,1,0:T(8,128)S(1)} %copy.11), channel_id=2, replica_groups=mesh['gx'=4,'gy'=4,'gz'=2] {'gx','gy','gz'}, dimensions={0}, use_global_device_ids=true | all-gather | bytes 52800 | tf_op jit(solution)/shard_map/all_gather | solution.py:118
  46.4 3.1 collective-permute-start.3
  51.9 5.0 collective-permute-done.2
  58.9 5.0 copy.10
  64.0 3.7 reshape_reshape.6
  72.7 13.2 %cholesky.18 = f32[128,128]{1,0:T(8,128)} custom-call(f32[128,128]{1,0:T(8,128)} %fusion.80), custom_call_target="Cholesky" | custom-call | tf_op jit(solution)/shard_map/jit(cholesky)/cholesky | solution.py:122
  91.1 3.3 convolution_bitcast_fusion.1
  97.2 4.0 collective-permute-start.7
  119.0 11.3 %custom-call.9 = f32[1,128,128]{1,2,0:T(8,128)} custom-call(f32[1,128,128]{2,1,0:T(8,128)} %fusion.71), custom_call_target="InvertDiagBlocksLowerTriangular" | custom-call | tf_op jit(solution)/shard_map/jit(_cho_solve)/triangular_solve | solution.py:148
  136.8 3.7 fusion.8
  140.5 36.0 %all-gather.6 = f32[32,20,128]{2,1,0:T(8,128)S(1)} all-gather(f32[1,20,128]{2,1,0:T(8,128)S(1)} %convolution_bitcast_fusion.7), channel_id=3, replica_groups=mesh['gx'=4,'gy'=4,'gz'=2] {'gx','gy','gz'}, dimensions={0}, use_global_device_ids=true | all-gather | bytes 337920 | tf_op jit(solution)/shard_map/all_gather | solution.py:125
  182.6 4.5 collective-permute-start.13
  203.3 7.4 %reduce.8 = f32[729,729]{1,0:T(8,128)} reduce(f32[1,1,1,729,729]{4,2,3,1,0:T(1,128)S(1)} %copy-done, f32[]{:T(128)} %constant.929), dimensions={0,1,2}, to_apply=%param.8.reduce_sub_computation | reduce | bytes 4251532 | tf_op args[1]
  210.7 3.7 reshape_reshape.7
  263.9 36.2 %all-gather.7 = f32[32,1,128]{2,1,0:T(1,128)} all-gather(f32[1,1,128]{2,1,0:T(1,128)S(1)} %bitcast.143), channel_id=4, replica_groups=mesh['gx'=4,'gy'=4,'gz'=2] {'gx','gy','gz'}, dimensions={0}, use_global_device_ids=true | all-gather | bytes 16896 | tf_op jit(solution)/shard_map/all_gather | solution.py:10
  301.5 43.6 %psum.14 = f32[128]{0:T(128)} all-reduce(f32[128]{0:T(128)} %get-tuple-element.3), channel_id=1, replica_groups=mesh['gx'=4,'gy'=4,'gz'=2] {'gx','gy','gz'}, use_global_device_ids=true, to_apply=%region_5.7 | all-reduce | flops 128 | bytes 1024 | tf_op jit(solution)/shard_map/psum | solution.py:177
  349.0 3.3 convolution_bitcast_fusion
  372.8 3.6 fusion.6
  376.8 37.3 %all-gather.8 = f32[32,20,128]{2,1,0:T(8,128)S(1)} all-gather(f32[1,20,128]{2,1,0:T(8,128)S(1)} %convolution_bitcast_fusion.6), channel_id=5, replica_groups=mesh['gx'=4,'gy'=4,'gz'=2] {'gx','gy','gz'}, dimensions={0}, use_global_device_ids=true | all-gather | bytes 337920 | tf_op jit(solution)/shard_map/all_gather | solution.py:125
  418.3 6.0 %collective-permute-start.31 = (f32[1,9,9,128]{3,2,1,0:T(8,128)S(1)}, f32[1,9,9,128]{3,2,1,0:T(8,128)S(1)}, u32[]{:S(2)}, u32[]{:S(2)}) collective-permute-start(f32[1,9,9,128]{3,2,1,0:T(8,128)S(1)} %get-tuple-element.14), channel_id=1, source_target_pairs={{8,0},{16,8},{24,16},{0,24},{9,1},{17,9},{25,17},{1,25},{10,2},{18... | collective-permute-start | bytes 124424 | tf_op jit(solution)/shard_map/ppermute | solution.py:23
  450.9 35.8 %all-gather.9 = f32[32,1,128]{2,1,0:T(1,128)S(1)} all-gather(f32[1,1,128]{2,1,0:T(1,128)S(1)} %bitcast.142), channel_id=6, replica_groups=mesh['gx'=4,'gy'=4,'gz'=2] {'gx','gy','gz'}, dimensions={0}, use_global_device_ids=true | all-gather | bytes 16896 | tf_op jit(solution)/shard_map/all_gather | solution.py:10
  494.5 4.8 collective-permute-start.37
  511.4 42.2 %psum.15 = f32[128]{0:T(128)S(1)} all-reduce(f32[128]{0:T(128)S(1)} %multiply_reduce_fusion), channel_id=1, replica_groups=mesh['gx'=4,'gy'=4,'gz'=2] {'gx','gy','gz'}, use_global_device_ids=true, to_apply=%region_9.11 | all-reduce | flops 128 | bytes 1024 | tf_op jit(solution)/shard_map/psum | solution.py:177
  (320 shorter events, 198.0 us)
Async XLA Ops:
  1.6 44.6 %collective-permute-start.1 = (f32[1,9,9,128]{3,2,1,0:T(8,128)S(1)}, f32[1,9,9,128]{3,2,1,0:T(8,128)S(1)}, u32[]{:S(2)}, u32[]{:S(2)}) collective-permute-start(f32[1,9,9,128]{3,2,1,0:T(8,128)S(1)} %get-tuple-element.38), channel_id=1, source_target_pairs={{8,0},{16,8},{24,16},{0,24},{9,1},{17,9},{25,17},{1,25},{10,2},{18... | collective-permute-start | bytes 124424 | tf_op jit(solution)/shard_map/ppermute | solution.py:23
  2.2 44.1 %collective-permute-start = (f32[1,9,9,128]{3,2,1,0:T(8,128)S(1)}, f32[1,9,9,128]{3,2,1,0:T(8,128)S(1)}, u32[]{:S(2)}, u32[]{:S(2)}) collective-permute-start(f32[1,9,9,128]{3,2,1,0:T(8,128)S(1)} %get-tuple-element.37), channel_id=1, source_target_pairs={{0,8},{8,16},{16,24},{24,0},{1,9},{9,17},{17,25},{25,1},{2,10},{10... | collective-permute-start | bytes 124424 | tf_op jit(solution)/shard_map/ppermute | solution.py:22
  46.4 5.5 collective-permute-start.3
  49.5 7.3 %collective-permute-start.2 = (f32[9,1,9,128]{3,2,1,0:T(8,128)S(1)}, f32[9,1,9,128]{3,2,1,0:T(8,128)S(1)}, u32[]{:S(2)}, u32[]{:S(2)}) collective-permute-start(f32[9,1,9,128]{3,2,1,0:T(8,128)S(1)} %get-tuple-element.35), channel_id=1, source_target_pairs={{0,2},{2,4},{4,6},{6,0},{1,3},{3,5},{5,7},{7,1},{8,10},{10,12},{12... | collective-permute-start | bytes 124424 | tf_op jit(solution)/shard_map/ppermute | solution.py:22
  57.7 28.2 %collective-permute-start.5 = (f32[9,9,1,128]{3,2,1,0:T(1,128)}, f32[9,9,1,128]{3,2,1,0:T(1,128)S(1)}, u32[]{:S(2)}, u32[]{:S(2)}) collective-permute-start(f32[9,9,1,128]{3,2,1,0:T(1,128)} %get-tuple-element.34), channel_id=1, source_target_pairs={{1,0},{0,1},{3,2},{2,3},{5,4},{4,5},{7,6},{6,7},{9,8},{8,9},{11,10... | collective-permute-start | bytes 124424 | tf_op jit(solution)/shard_map/ppermute | solution.py:23
  57.7 28.2 %collective-permute-start.4 = (f32[9,9,1,128]{3,2,1,0:T(1,128)}, f32[9,9,1,128]{3,2,1,0:T(1,128)}, u32[]{:S(2)}, u32[]{:S(2)}) collective-permute-start(f32[9,9,1,128]{3,2,1,0:T(1,128)} %get-tuple-element.33), channel_id=1, source_target_pairs={{0,1},{1,0},{2,3},{3,2},{4,5},{5,4},{6,7},{7,6},{8,9},{9,8},{10,11... | collective-permute-start | bytes 124424 | tf_op jit(solution)/shard_map/ppermute | solution.py:22
  97.2 8.7 %collective-permute-start.7 = (f32[1,9,9,128]{3,2,1,0:T(8,128)}, f32[1,9,9,128]{3,2,1,0:T(8,128)}, u32[]{:S(2)}, u32[]{:S(2)}) collective-permute-start(f32[1,9,9,128]{3,2,1,0:T(8,128)} %slice.187), channel_id=1, source_target_pairs={{8,0},{16,8},{24,16},{0,24},{9,1},{17,9},{25,17},{1,25},{10,2},{18... | collective-permute-start | bytes 124424 | tf_op jit(solution)/shard_map/ppermute | solution.py:23
  102.7 4.7 collective-permute-start.6
  108.6 5.1 collective-permute-start.9
  117.2 13.8 %collective-permute-start.11 = (f32[9,9,1,128]{3,2,1,0:T(1,128)}, f32[9,9,1,128]{3,2,1,0:T(1,128)}, u32[]{:S(2)}, u32[]{:S(2)}) collective-permute-start(f32[9,9,1,128]{3,2,1,0:T(1,128)} %get-tuple-element.30), channel_id=1, source_target_pairs={{1,0},{0,1},{3,2},{2,3},{5,4},{4,5},{7,6},{6,7},{9,8},{8,9},{11,10... | collective-permute-start | bytes 124424 | tf_op jit(solution)/shard_map/ppermute | solution.py:23
  117.2 13.8 %collective-permute-start.10 = (f32[9,9,1,128]{3,2,1,0:T(1,128)}, f32[9,9,1,128]{3,2,1,0:T(1,128)}, u32[]{:S(2)}, u32[]{:S(2)}) collective-permute-start(f32[9,9,1,128]{3,2,1,0:T(1,128)} %get-tuple-element.29), channel_id=1, source_target_pairs={{0,1},{1,0},{2,3},{3,2},{4,5},{5,4},{6,7},{7,6},{8,9},{9,8},{10,11... | collective-permute-start | bytes 124424 | tf_op jit(solution)/shard_map/ppermute | solution.py:22
  182.6 7.6 %collective-permute-start.13 = (f32[1,9,9,128]{3,2,1,0:T(8,128)S(1)}, f32[1,9,9,128]{3,2,1,0:T(8,128)S(1)}, u32[]{:S(2)}, u32[]{:S(2)}) collective-permute-start(f32[1,9,9,128]{3,2,1,0:T(8,128)S(1)} %get-tuple-element.28), channel_id=1, source_target_pairs={{8,0},{16,8},{24,16},{0,24},{9,1},{17,9},{25,17},{1,25},{10,2},{18... | collective-permute-start | bytes 124424 | tf_op jit(solution)/shard_map/ppermute | solution.py:23
  202.1 21.0 %collective-permute-start.17 = (f32[9,9,1,128]{3,2,1,0:T(1,128)}, f32[9,9,1,128]{3,2,1,0:T(1,128)}, u32[]{:S(2)}, u32[]{:S(2)}) collective-permute-start(f32[9,9,1,128]{3,2,1,0:T(1,128)} %get-tuple-element.24), channel_id=1, source_target_pairs={{1,0},{0,1},{3,2},{2,3},{5,4},{4,5},{7,6},{6,7},{9,8},{8,9},{11,10... | collective-permute-start | bytes 124424 | tf_op jit(solution)/shard_map/ppermute | solution.py:23
  202.1 21.0 %collective-permute-start.16 = (f32[9,9,1,128]{3,2,1,0:T(1,128)}, f32[9,9,1,128]{3,2,1,0:T(1,128)}, u32[]{:S(2)}, u32[]{:S(2)}) collective-permute-start(f32[9,9,1,128]{3,2,1,0:T(1,128)} %get-tuple-element.23), channel_id=1, source_target_pairs={{0,1},{1,0},{2,3},{3,2},{4,5},{5,4},{6,7},{7,6},{8,9},{9,8},{10,11... | collective-permute-start | bytes 124424 | tf_op jit(solution)/shard_map/ppermute | solution.py:22
  242.4 6.7 %collective-permute-start.19 = (f32[1,9,9,128]{3,2,1,0:T(8,128)}, f32[1,9,9,128]{3,2,1,0:T(8,128)}, u32[]{:S(2)}, u32[]{:S(2)}) collective-permute-start(f32[1,9,9,128]{3,2,1,0:T(8,128)} %slice.202), channel_id=1, source_target_pairs={{8,0},{16,8},{24,16},{0,24},{9,1},{17,9},{25,17},{1,25},{10,2},{18... | collective-permute-start | bytes 124424 | tf_op jit(solution)/shard_map/ppermute | solution.py:23
  246.5 5.1 collective-permute-start.18
  252.8 5.1 collective-permute-start.21
  353.1 5.6 %collective-permute-start.25 = (f32[1,9,9,128]{3,2,1,0:T(8,128)}, f32[1,9,9,128]{3,2,1,0:T(8,128)}, u32[]{:S(2)}, u32[]{:S(2)}) collective-permute-start(f32[1,9,9,128]{3,2,1,0:T(8,128)} %slice.211), channel_id=1, source_target_pairs={{8,0},{16,8},{24,16},{0,24},{9,1},{17,9},{25,17},{1,25},{10,2},{18... | collective-permute-start | bytes 124424 | tf_op jit(solution)/shard_map/ppermute | solution.py:23
  353.8 5.2 collective-permute-start.24
  360.2 5.1 collective-permute-start.27
  362.1 4.7 collective-permute-start.26
  418.3 9.7 %collective-permute-start.31 = (f32[1,9,9,128]{3,2,1,0:T(8,128)S(1)}, f32[1,9,9,128]{3,2,1,0:T(8,128)S(1)}, u32[]{:S(2)}, u32[]{:S(2)}) collective-permute-start(f32[1,9,9,128]{3,2,1,0:T(8,128)S(1)} %get-tuple-element.14), channel_id=1, source_target_pairs={{8,0},{16,8},{24,16},{0,24},{9,1},{17,9},{25,17},{1,25},{10,2},{18... | collective-permute-start | bytes 124424 | tf_op jit(solution)/shard_map/ppermute | solution.py:23
  430.2 5.1 collective-permute-start.32
  494.5 8.4 %collective-permute-start.37 = (f32[1,9,9,128]{3,2,1,0:T(8,128)S(1)}, f32[1,9,9,128]{3,2,1,0:T(8,128)S(1)}, u32[]{:S(2)}, u32[]{:S(2)}) collective-permute-start(f32[1,9,9,128]{3,2,1,0:T(8,128)S(1)} %slice.225), channel_id=1, source_target_pairs={{8,0},{16,8},{24,16},{0,24},{9,1},{17,9},{25,17},{1,25},{10,2},{18... | collective-permute-start | bytes 124424 | tf_op jit(solution)/shard_map/ppermute | solution.py:23
  (70 other events, 870.3 us)
